TPU v7x, 512 devices: a whole 4x8x8 slice. The times are simulated.
512 devices in a mesh: ladder: 16 (over y, z_lo), grp: 32 (over x, z_hi, core).
Axes of the slice: x: 4, y: 8, z: 8 (z_hi: 4, z_lo: 2; z = z_hi * 2 + z_lo), core: 2. Of those that a mesh axis runs over, the one named last changes fastest.
Arguments:
- init_up: int32 [8192, 144], P(('ladder', 'grp')), may hold values 0 or 1
- flip_site: int32 [4, 8192], P(None, ('ladder', 'grp')), may hold values from 0 to 143
- accept: int32 [4, 8192], P(None, ('ladder', 'grp')), may hold values from 0 to 1
- swap_ok: int32 [4, 8, 512], P(None, None, 'grp'), may hold values 0 or 1
- ladder_bit: int32 [4, 32], P(None, 'grp'), may hold values from 0 to 3
- w_embed: bfloat16 [4, 72], replicated, may hold values from -3 to 3
- pos_embed: float32 [36, 72], replicated, may hold values from -6 to 6
- w_value: bfloat16 [2, 72, 72], replicated, may hold values from -0.75 to 0.75
- mixing: float32 [2, 12, 36, 36], replicated, may hold values from -1 to 1
- w_out: bfloat16 [2, 72, 72], replicated, may hold values from -0.75 to 0.75
- w_in: bfloat16 [2, 72, 288], replicated, may hold values from -0.75 to 0.75
- w_back: bfloat16 [2, 288, 72], replicated, may hold values from -0.375 to 0.375
- w_final: float32 [72, 72], replicated, may hold values from -0.75 to 0.75
- b_final: float32 [72], replicated, may hold values from -5 to 5
Outputs:
- proposal_amp: float32 [4, 8192], P(None, ('ladder', 'grp'))
- final_spins: float32 [8192, 144], P(('ladder', 'grp'))
- final_amp: float32 [8192], P(('ladder', 'grp'))
- accept_counts: float32 [16, 4], P('ladder')
All inputs are finite; a program needn't handle non-finite values. No bound on the sum of `init_up` or of `swap_ok` on one device may be relied on, other than what follows from the above.
Results may differ from a plain program's by a relative error of at most 0.002.
Values sent between devices are 32-bit elements; how exact they have to be, the bound alone decides.
No kernel may reach another device: no remote copies, remote signals or barrier semaphores. Data moves between devices by JAX's collectives and lax.ppermute only.
A program may use at most 64 MiB of HBM per device.

v0:
```python
import jax
import jax.numpy as jnp
import numpy as np
from jax import lax
from jax.experimental import pallas as pl
from jax.experimental.pallas import tpu as pltpu
from jax.sharding import PartitionSpec as P


SIDE = 12
SITES = 144
PATCHES = 36
D = 72
HEADS = 12
HEAD_DIM = 6
HID = 288
LAYERS = 2
STEPS = 4
PAIRS = 8
RUNGS = 16
PLACES = 16

PACK = 7
LANES = 256
CHAINS = (STEPS + 1) * PLACES
GROUPS = -(-CHAINS // PACK)
ROWS = 96
SLOT = 8
HD = HEADS * SLOT
MSG = SITES + 2 * STEPS
GELU_A = float(np.sqrt(2.0 / np.pi))
GELU_B = GELU_A * 0.044715


def constants():
    lane = np.arange(LANES)
    used = lane < PACK * PATCHES
    patch = lane % PATCHES
    chain = lane // PATCHES
    spread = (np.arange(PATCHES)[:, None] == patch[None, :]) & used[None, :]
    block = (chain[:, None] == chain[None, :]) & used[:, None] & used[None, :]
    pick = np.zeros((SITES, 4 * LANES), np.float32)
    for row in range(2):
        for column in range(2):
            site = (2 * (patch // 6) + row) * SIDE + 2 * (patch % 6) + column
            pick[:, (row * 2 + column) * LANES : (row * 2 + column + 1) * LANES] = (
                np.arange(SITES)[:, None] == site[None, :]
            ) & used[None, :]
    pool = (chain[:, None] == np.arange(128)[None, :]) & used[:, None]
    pad = np.zeros((HD, D), np.float32)
    for head in range(HEADS):
        for entry in range(HEAD_DIM):
            pad[head * SLOT + entry, head * HEAD_DIM + entry] = 1.0
    repeat = np.zeros((4, 64), np.float32)
    for s in range(4):
        repeat[s, s * 16 : (s + 1) * 16] = 1.0
    low = jnp.bfloat16
    return (
        jnp.asarray(spread, low),
        jnp.asarray(spread.T, low),
        jnp.asarray(block, jnp.float32),
        jnp.asarray(pick, low),
        jnp.asarray(pool, low),
        jnp.asarray(pad, low),
        jnp.asarray(repeat, low),
    )


def mm(a, b):
    return jnp.dot(a, b, preferred_element_type=jnp.float32)


def mm_t(a, b):
    return lax.dot_general(a, b, (((1,), (1,)), ((), ())), preferred_element_type=jnp.float32)


def exact(a, b):
    return jnp.dot(a, b, preferred_element_type=jnp.float32, precision=lax.Precision.HIGHEST)


def norm(x):
    center = x - jnp.sum(x, axis=0, keepdims=True) * (1.0 / D)
    spread = jnp.sum(center * center, axis=0, keepdims=True) * (1.0 / D)
    return center * lax.rsqrt(spread + 1e-05)


def kernel(
    bit_hbm,
    got_ref,
    swap_ref,
    small_ref,
    pos_ref,
    w_value_ref,
    mixing_ref,
    w_out_ref,
    w_in_ref,
    w_back_ref,
    w_final_ref,
    spread_ref,
    spread_t_ref,
    block_ref,
    pick_ref,
    pool_ref,
    pad_ref,
    repeat_ref,
    prop_ref,
    spins_ref,
    amp_ref,
    state,
    chains,
    picked,
    pos_x,
    embed_x,
    wv,
    wo,
    wi,
    wb,
    big,
    stream,
    normed,
    rests,
    hidden,
    value,
    mixed,
    bit_ref,
    arrived,
):
    low = jnp.bfloat16
    me = lax.axis_index("ladder")
    copy = pltpu.make_async_copy(bit_hbm, bit_ref, arrived)
    copy.start()

    pos_x[...] = exact(pos_ref[...].T, spread_ref[...].astype(jnp.float32))
    for layer in range(LAYERS):
        wv[layer] = mm_t(pad_ref[...], w_value_ref[layer]).astype(low)
        wo[layer] = mm(pad_ref[...], w_out_ref[layer]).T.astype(low)
        wi[layer] = w_in_ref[layer].astype(jnp.float32).T.astype(low)
        wb[layer] = (0.5 * w_back_ref[layer].astype(jnp.float32)).T.astype(low)
    for layer in range(LAYERS):
        for head in range(HEADS):
            one = mixing_ref[layer, head]
            twice = jnp.concatenate([one, one], axis=1).T.astype(low)
            wide = mm(twice, spread_ref[...])
            for half in range(2):
                lanes = slice(half * 128, half * 128 + 128)
                tiles = []
                for start in range(0, LANES, 2 * PATCHES):
                    rows = min(2 * PATCHES, LANES - start)
                    end = min(start + 2 * PATCHES, PACK * PATCHES)
                    if end <= half * 128 or start >= half * 128 + 128:
                        tiles.append(jnp.zeros((rows, 128), jnp.float32))
                    else:
                        tiles.append(wide[:rows, lanes] * block_ref[start : start + rows, lanes])
                big[layer, head, :, lanes] = jnp.concatenate(tiles, axis=0).astype(low)

    copy.wait()
    embed_x[...] = mm(small_ref[:4].T.astype(low), repeat_ref[...]).astype(low)

    column = lax.broadcasted_iota(jnp.int32, (PLACES, SITES), 1).astype(jnp.float32)
    for rung in range(RUNGS):
        state[rung] = got_ref[rung, :, :SITES]
    chains[CHAINS:, :] = jnp.zeros((ROWS - CHAINS, SITES), jnp.float32)
    for step in range(STEPS):
        own_site = got_ref[me, :, SITES + step : SITES + step + 1]
        own = state[me]
        chains[step * PLACES : (step + 1) * PLACES, :] = jnp.where(column == own_site, -own, own)
        bit = bit_ref[step, 0]
        mask = jnp.left_shift(jnp.int32(1), bit)
        decided = swap_ref[step].T
        for rung in range(RUNGS):
            site = got_ref[rung, :, SITES + step : SITES + step + 1]
            taken = got_ref[rung, :, SITES + STEPS + step : SITES + STEPS + step + 1]
            flip = jnp.where(taken > 0.5, site, -1.0)
            now = state[rung]
            state[rung] = jnp.where(column == flip, -now, now)
        for pair in range(PAIRS):
            lower = jnp.left_shift(jnp.right_shift(jnp.int32(pair), bit), bit + 1) + jnp.bitwise_and(
                jnp.int32(pair), mask - 1
            )
            upper = lower + mask
            ok = decided[:, pair : pair + 1] == 1
            a, b = state[lower], state[upper]
            state[lower] = jnp.where(ok, b, a)
            state[upper] = jnp.where(ok, a, b)
    last = state[me]
    spins_ref[...] = last
    chains[STEPS * PLACES : CHAINS, :] = last

    picked[...] = mm(chains[...].astype(low), pick_ref[...])
    lane = lax.broadcasted_iota(jnp.int32, (16, LANES), 1)
    row = lax.broadcasted_iota(jnp.int32, (16, LANES), 0)
    slot = sum((lane >= PATCHES * k).astype(jnp.int32) for k in range(1, PACK + 1))

    def to_value(layer):
        for pair in range(GROUPS // 2):
            one = mm(wv[layer], normed[2 * pair])
            two = mm(wv[layer], normed[2 * pair + 1])
            for head in range(HEADS):
                rows = slice(head * SLOT, (head + 1) * SLOT)
                both = jnp.concatenate([one[rows], two[rows]], axis=0)
                value[head, pair * 2 * SLOT : (pair + 1) * 2 * SLOT, :] = both.astype(low)

    def mix(layer):
        for pair in range(HEADS // 2):
            one = mm(value[2 * pair], big[layer, 2 * pair])
            two = mm(value[2 * pair + 1], big[layer, 2 * pair + 1])
            for group in range(GROUPS):
                rows = slice(group * SLOT, (group + 1) * SLOT)
                both = jnp.concatenate([one[rows], two[rows]], axis=0)
                mixed[group, pair * 2 * SLOT : (pair + 1) * 2 * SLOT, :] = both.astype(low)

    for group in range(GROUPS):
        first = PACK * group // 8 * 8
        mine = slot + (PACK * group - first) == row
        parts = [
            jnp.where(mine, picked[first : first + 16, s * LANES : (s + 1) * LANES], 0.0) for s in range(4)
        ]
        x = mm(embed_x[...], jnp.concatenate(parts, axis=0).astype(low)) + pos_x[...]
        stream[group] = x
        normed[group] = norm(x).astype(low)

    for layer in range(LAYERS):
        to_value(layer)
        mix(layer)
        for group in range(GROUPS):
            x = stream[group] + mm(wo[layer], mixed[group])
            stream[group] = x
            normed[group] = norm(x).astype(low)
        for group in range(GROUPS):
            h = mm(wi[layer], normed[group]).astype(low)
            hidden[group] = h + h * jnp.tanh(h * (low(GELU_B) * (h * h) + low(GELU_A)))
        for group in range(GROUPS):
            x = stream[group] + mm(wb[layer], hidden[group])
            if layer + 1 < LAYERS:
                stream[group] = x
                normed[group] = norm(x).astype(low)
            else:
                x = norm(x)
                high = x.astype(low)
                normed[group] = high
                rests[group] = (x - high.astype(jnp.float32)).astype(low)
    total = jnp.zeros((D, 128), jnp.float32)
    for group in range(GROUPS):
        part = mm(normed[group], pool_ref[...]) + mm(rests[group], pool_ref[...])
        total = total + (part if group == 0 else pltpu.roll(part, PACK * group, 1))

    eye = lax.broadcasted_iota(jnp.int32, (D, D), 0) == lax.broadcasted_iota(jnp.int32, (D, D), 1)
    bias = jnp.sum(jnp.where(eye, small_ref[4:5], 0.0), axis=1, keepdims=True)
    heads = exact(w_final_ref[...].T, total * (2.0 / SIDE)) + bias
    size = jnp.abs(heads)
    log_cosh = size + jnp.log1p(jnp.exp(-2.0 * size)) - float(np.log(2.0))
    amps = jnp.sum(log_cosh, axis=0, keepdims=True) * (1.0 / D)
    for step in range(STEPS):
        prop_ref[step : step + 1, :] = amps[:, step * PLACES : (step + 1) * PLACES]
    amp_ref[...] = amps[:, STEPS * PLACES : CHAINS]


def from_everyone(shard, axis):
    size = lax.axis_size(axis)
    return lax.all_to_all(
        jnp.broadcast_to(shard[None], (size, *shard.shape)), axis, 0, 0, tiled=True
    )


def on_device(
    init_up,
    flip_site,
    accept,
    swap_ok,
    ladder_bit,
    w_embed,
    pos_embed,
    w_value,
    mixing,
    w_out,
    w_in,
    w_back,
    w_final,
    b_final,
):
    f32, low = jnp.float32, jnp.bfloat16
    marks = jnp.concatenate([flip_site, accept], axis=0).astype(f32).T
    message = jnp.concatenate([2.0 * init_up.astype(f32) - 1.0, marks], axis=1)
    got = from_everyone(message, "ladder")
    got = got.reshape(RUNGS, PLACES, MSG)
    local_counts = jnp.sum(accept.astype(f32), axis=1)
    vmem = pl.BlockSpec(memory_space=pltpu.VMEM)
    hbm = pl.BlockSpec(memory_space=pltpu.HBM)
    replay = pl.pallas_call(
        kernel,
        out_shape=(
            jax.ShapeDtypeStruct((STEPS, PLACES), f32),
            jax.ShapeDtypeStruct((PLACES, SITES), f32),
            jax.ShapeDtypeStruct((1, PLACES), f32),
        ),
        in_specs=[hbm] + [vmem] * 17,
        out_specs=(vmem, vmem, vmem),
        scratch_shapes=[
            pltpu.VMEM((RUNGS, PLACES, SITES), f32),
            pltpu.VMEM((ROWS, SITES), f32),
            pltpu.VMEM((ROWS, 4 * LANES), f32),
            pltpu.VMEM((D, LANES), f32),
            pltpu.VMEM((D, 64), low),
            pltpu.VMEM((LAYERS, HD, D), low),
            pltpu.VMEM((LAYERS, D, HD), low),
            pltpu.VMEM((LAYERS, HID, D), low),
            pltpu.VMEM((LAYERS, D, HID), low),
            pltpu.VMEM((LAYERS, HEADS, LANES, LANES), low),
            pltpu.VMEM((GROUPS, D, LANES), f32),
            pltpu.VMEM((GROUPS, D, LANES), low),
            pltpu.VMEM((GROUPS, D, LANES), low),
            pltpu.VMEM((GROUPS, HID, LANES), low),
            pltpu.VMEM((HEADS, ROWS, LANES), low),
            pltpu.VMEM((GROUPS, HD, LANES), low),
            pltpu.SMEM((STEPS, 1), jnp.int32),
            pltpu.SemaphoreType.DMA,
        ],
        compiler_params=pltpu.CompilerParams(vmem_limit_bytes=40 * 1024 * 1024),
        cost_estimate=pl.CostEstimate(flops=2 * 10**9, bytes_accessed=10**6, transcendentals=10**6),
    )
    small = jnp.concatenate([w_embed.astype(f32), b_final[None]], axis=0)
    inputs = (
        ladder_bit,
        got,
        swap_ok,
        small,
        pos_embed,
        w_value,
        mixing,
        w_out,
        w_in,
        w_back,
        w_final,
        *constants(),
    )
    prop, spins, amp = replay(*inputs)
    size = lax.axis_size("grp")
    other = lax.ppermute(local_counts, "grp", [(g, g ^ 1) for g in range(size)])
    both = local_counts + other
    shares = jnp.broadcast_to(both[None, None], (size // 2, 1, STEPS))
    groups = [list(range(core, size, 2)) for core in range(2)]
    shares = lax.all_to_all(shares, "grp", 0, 0, tiled=True, axis_index_groups=groups)
    totals = shares.sum(axis=(0, 1))
    return (prop, spins, amp.reshape(PLACES), totals.reshape(1, -1))


def solution(mesh):
    placed = (
        P(("ladder", "grp"), None),
        P(None, ("ladder", "grp")),
        P(None, ("ladder", "grp")),
        P(None, None, "grp"),
        P(None, "grp"),
        P(),
        P(),
        P(),
        P(),
        P(),
        P(),
        P(),
        P(),
        P(),
    )
    return jax.shard_map(
        on_device,
        mesh=mesh,
        in_specs=placed,
        out_specs=(
            P(None, ("ladder", "grp")),
            P(("ladder", "grp"), None),
            P(("ladder", "grp")),
            P("ladder", None),
        ),
        check_vma=False,
    )
```

profile of v0, /device:TPU:2, one launch (start us, length us, event | category | flops | bytes accessed | tf_op | source)
XLA Modules:
  0.0 54.9 jit_solution(161918926270027548)
XLA Ops:
  0.6 0.0 copy-start.16
  0.6 0.0 copy-start.15
  0.7 0.8 %convert_reduce_fusion = f32[4]{0:T(128)S(1)} fusion(s32[4,16]{1,0:T(4,128)} %param.23), kind=kLoop, calls=%fused_computation.5 | loop fusion | flops 124 | bytes 272 | tf_op jit(solution)/shard_map/reduce_sum | solution.py:286
  1.5 1.9 %collective-permute-start = (f32[4]{0:T(128)S(1)}, f32[4]{0:T(128)S(1)}, u32[]{:S(2)}, u32[]{:S(2)}) collective-permute-start(f32[4]{0:T(128)S(1)} %convert_reduce_fusion), channel_id=1, source_target_pairs={{0,1},{1,0},{2,3},{3,2},{4,5},{5,4},{6,7},{7,6},{8,9},{9,8},{10,11... | collective-permute-start | bytes 56 | tf_op jit(solution)/shard_map/ppermute | solution.py:338
  3.4 0.0 copy-done.16
  3.4 0.7 %fusion = f32[16,8]{0,1:T(8,128)S(1)} fusion(s32[4,16]{1,0:T(4,128)S(1)} %copy-done.16, s32[4,16]{1,0:T(4,128)} %param.22), kind=kLoop, calls=%fused_computation.3 | loop fusion | flops 256 | bytes 1024 | tf_op jit(solution)/shard_map/transpose | solution.py:282
  4.1 0.1 copy.33
  4.2 0.0 copy-done.15
  4.2 0.0 copy-start.13
  4.2 0.3 collective-permute-done
  4.6 0.6 %broadcast_in_dim.8 = f32[16,1,4]{2,1,0:T(1,128)} broadcast(f32[4]{0:T(128)S(1)} %add.4), dimensions={2} | broadcast | bytes 272 | tf_op jit(solution)/shard_map/broadcast_in_dim | solution.py:340
  5.2 13.3 %all-to-all-start.1 = ((f32[16,1,4]{2,1,0:T(1,128)}), f32[16,1,4]{2,1,0:T(1,128)S(1)}, u32[]{:S(2)}, u32[]{:S(2)}) async-start(f32[16,1,4]{2,1,0:T(1,128)} %broadcast_in_dim.8), calls=%async_computation.1 | async-start | bytes 16384 | tf_op jit(solution)/shard_map/all_to_all | solution.py:342
  18.5 0.1 pad_maximum_fusion
  18.5 8.5 %all-to-all-done.1 = f32[16,1,4]{2,1,0:T(1,128)S(1)} async-done(((f32[16,1,4]{2,1,0:T(1,128)}), f32[16,1,4]{2,1,0:T(1,128)S(1)}, u32[]{:S(2)}, u32[]{:S(2)}) %all-to-all-start.1) | async-done | bytes 288 | tf_op jit(solution)/shard_map/all_to_all | solution.py:342
  27.0 0.7 %broadcast_in_dim.6 = f32[16,16,152]{2,1,0:T(8,128)} broadcast(f32[16,152]{1,0:T(8,128)S(1)} %pad_maximum_fusion), dimensions={1,2} | broadcast | bytes 165376 | tf_op jit(solution)/shard_map/broadcast_in_dim | solution.py:261
  27.8 8.2 %all-to-all-start = ((f32[16,16,152]{2,1,0:T(8,128)}), f32[16,16,152]{2,1,0:T(8,128)S(1)}, u32[]{:S(2)}, u32[]{:S(2)}) async-start(f32[16,16,152]{2,1,0:T(8,128)} %broadcast_in_dim.6), calls=%async_computation | async-start | bytes 524288 | tf_op jit(solution)/shard_map/all_to_all | solution.py:260
  36.0 0.0 copy-done.18
  36.0 0.0 copy-start.17
  36.0 0.1 copy.34.bit_hbm
  36.1 0.6 %copy-done.17 = bf16[4,72]{1,0:T(4,128)(2,1)S(1)} copy-done((bf16[4,72]{1,0:T(4,128)(2,1)S(1)}, bf16[4,72]{1,0:T(4,128)(2,1)}, u32[]{:S(2)}) %copy-start.17) | copy-done | bytes 600
  36.7 0.0 copy-done.13
  36.7 0.0 copy-start.7
  36.7 0.0 copy-start.8
  36.7 0.0 copy-start.9
  36.8 0.0 copy-start.10
  36.8 0.0 copy-start.11
  36.8 0.8 %copy-done.14 = bf16[2,288,72]{1,2,0:T(8,128)(2,1)S(1)} copy-done((bf16[2,288,72]{1,2,0:T(8,128)(2,1)S(1)}, bf16[2,288,72]{1,2,0:T(8,128)(2,1)}, u32[]{:S(2)}) %copy-start.14) | copy-done | bytes 82968
  37.6 0.0 copy-start.3
  37.6 0.0 copy-start.4
  37.6 0.2 copy.36.w_back_ref
  37.8 0.0 copy-start.5
  37.8 0.4 copy-done.19
  38.3 0.5 reduce_sum.19
  38.8 8.3 %all-to-all-done.got_ref = f32[16,16,152]{2,1,0:T(8,128)S(1)} async-done(((f32[16,16,152]{2,1,0:T(8,128)}), f32[16,16,152]{2,1,0:T(8,128)S(1)}, u32[]{:S(2)}, u32[]{:S(2)}) %all-to-all-start) | async-done | bytes 155680 | tf_op jit(solution)/shard_map/all_to_all | solution.py:260
  47.1 0.0 copy-done.6
  47.1 0.0 copy-done.7
  47.1 0.0 copy-done.8
  47.1 0.0 copy-done.9
  47.1 0.0 copy-done.10
  47.1 0.0 copy-done.11
  47.1 0.0 copy-done
  47.1 0.0 copy-done.1
  47.1 0.0 copy-done.2
  47.2 0.0 copy-done.3
  47.2 0.0 copy-done.4
  47.2 0.0 copy-done.5
  47.2 0.0 copy-done.12
  47.2 7.7 %shard_map.228 = (f32[4,16]{1,0:T(4,128)}, f32[16,144]{1,0:T(8,128)}, f32[1,16]{1,0:T(1,128)}) custom-call(s32[4,1]{1,0:T(4,128)S(1)} %copy.34.bit_hbm, f32[16,16,152]{2,1,0:T(8,128)S(1)} %all-to-all-done.got_ref, s32[4,8,16]{2,1,0:T(8,128)S(1)} %copy-done.5, f32[5,72]{1,0:T(8,128)S(1)} %pad_maximum_fusion.1.small_ref, f32[36,72]{1,0:T(8,128)S(1)} %copy-done.4, ...), custom_call_target="tpu_custom_call" | custom-call | flops 2000000000 | bytes 1000000 | tf_op jit(solution)/shard_map/pallas_call | solution.py:336
  (13 shorter events, 0.1 us)
Async XLA Ops:
  0.6 2.8 %copy-start.16 = (s32[4,16]{1,0:T(4,128)S(1)}, s32[4,16]{1,0:T(4,128)}, u32[]{:S(2)}) copy-start(s32[4,16]{1,0:T(4,128)} %param.23) | copy-start | bytes 772
  0.6 3.6 %copy-start.15 = (s32[16,144]{1,0:T(8,128)S(1)}, s32[16,144]{1,0:T(8,128)}, u32[]{:S(2)}) copy-start(s32[16,144]{1,0:T(8,128)} %param.21) | copy-start | bytes 27652
  1.5 3.0 %collective-permute-start = (f32[4]{0:T(128)S(1)}, f32[4]{0:T(128)S(1)}, u32[]{:S(2)}, u32[]{:S(2)}) collective-permute-start(f32[4]{0:T(128)S(1)} %convert_reduce_fusion), channel_id=1, source_target_pairs={{0,1},{1,0},{2,3},{3,2},{4,5},{5,4},{6,7},{7,6},{8,9},{9,8},{10,11... | collective-permute-start | bytes 56 | tf_op jit(solution)/shard_map/ppermute | solution.py:338
  4.2 32.5 %copy-start.13 = (f32[2,12,36,36]{3,0,2,1:T(2,128)S(1)}, f32[2,12,36,36]{3,0,2,1:T(2,128)}, u32[]{:S(2)}) copy-start(f32[2,12,36,36]{3,0,2,1:T(2,128)} %param.29) | copy-start | bytes 373252
  5.2 21.9 %all-to-all-start.1 = ((f32[16,1,4]{2,1,0:T(1,128)}), f32[16,1,4]{2,1,0:T(1,128)S(1)}, u32[]{:S(2)}, u32[]{:S(2)}) async-start(f32[16,1,4]{2,1,0:T(1,128)} %broadcast_in_dim.8), calls=%async_computation.1 | async-start | bytes 16384 | tf_op jit(solution)/shard_map/all_to_all | solution.py:342
  27.7 8.3 %copy-start.18 = (s32[4,1]{0,1:T(1,128)S(1)}, s32[4,1]{0,1:T(1,128)}, u32[]{:S(2)}) copy-start(s32[4,1]{0,1:T(1,128)} %param.25) | copy-start | bytes 52
  27.8 19.3 %all-to-all-start = ((f32[16,16,152]{2,1,0:T(8,128)}), f32[16,16,152]{2,1,0:T(8,128)S(1)}, u32[]{:S(2)}, u32[]{:S(2)}) async-start(f32[16,16,152]{2,1,0:T(8,128)} %broadcast_in_dim.6), calls=%async_computation | async-start | bytes 524288 | tf_op jit(solution)/shard_map/all_to_all | solution.py:260
  36.0 0.7 %copy-start.17 = (bf16[4,72]{1,0:T(4,128)(2,1)S(1)}, bf16[4,72]{1,0:T(4,128)(2,1)}, u32[]{:S(2)}) copy-start(bf16[4,72]{1,0:T(4,128)(2,1)} %param.26) | copy-start | bytes 1732
  36.7 0.9 %copy-start.14 = (bf16[2,288,72]{1,2,0:T(8,128)(2,1)S(1)}, bf16[2,288,72]{1,2,0:T(8,128)(2,1)}, u32[]{:S(2)}) copy-start(bf16[2,288,72]{1,2,0:T(8,128)(2,1)} %param.32) | copy-start | bytes 248836
  36.7 10.4 %copy-start.6 = (bf16[144,1024]{1,0:T(8,128)(2,1)S(1)}, bf16[144,1024]{1,0:T(8,128)(2,1)}, u32[]{:S(2)}) copy-start(bf16[144,1024]{1,0:T(8,128)(2,1)} %constant.24.clone.pick_ref) | copy-start | bytes 884740
  36.7 10.4 %copy-start.7 = (f32[256,256]{1,0:T(8,128)S(1)}, f32[256,256]{1,0:T(8,128)}, u32[]{:S(2)}) copy-start(f32[256,256]{1,0:T(8,128)} %constant.23.clone.block_ref) | copy-start | bytes 786436
  36.7 10.4 %copy-start.8 = (bf16[256,36]{1,0:T(8,128)(2,1)S(1)}, bf16[256,36]{1,0:T(8,128)(2,1)}, u32[]{:S(2)}) copy-start(bf16[256,36]{1,0:T(8,128)(2,1)} %constant.22.clone.spread_t_ref) | copy-start | bytes 55300
  36.7 10.4 %copy-start.9 = (bf16[256,128]{1,0:T(8,128)(2,1)S(1)}, bf16[256,128]{1,0:T(8,128)(2,1)}, u32[]{:S(2)}) copy-start(bf16[256,128]{1,0:T(8,128)(2,1)} %constant.25.clone.pool_ref) | copy-start | bytes 196612
  36.8 10.4 %copy-start.10 = (bf16[96,72]{1,0:T(8,128)(2,1)S(1)}, bf16[96,72]{1,0:T(8,128)(2,1)}, u32[]{:S(2)}) copy-start(bf16[96,72]{1,0:T(8,128)(2,1)} %constant.26.clone.pad_ref) | copy-start | bytes 41476
  36.8 10.4 %copy-start.11 = (bf16[36,256]{1,0:T(8,128)(2,1)S(1)}, bf16[36,256]{1,0:T(8,128)(2,1)}, u32[]{:S(2)}) copy-start(bf16[36,256]{1,0:T(8,128)(2,1)} %constant.21.clone.spread_ref) | copy-start | bytes 55300
  37.6 0.7 %copy-start.19 = (f32[72]{0:T(128)S(1)}, f32[72]{0:T(128)}, u32[]{:S(2)}) copy-start(f32[72]{0:T(128)} %param.34) | copy-start | bytes 868
  37.6 9.5 %copy-start = (bf16[2,72,288]{2,1,0:T(8,128)(2,1)S(1)}, bf16[2,72,288]{2,1,0:T(8,128)(2,1)}, u32[]{:S(2)}) copy-start(bf16[2,72,288]{2,1,0:T(8,128)(2,1)} %w_in_ref.1) | copy-start | bytes 248836
  37.6 9.5 %copy-start.1 = (bf16[2,72,72]{2,1,0:T(8,128)(2,1)S(1)}, bf16[2,72,72]{2,1,0:T(8,128)(2,1)}, u32[]{:S(2)}) copy-start(bf16[2,72,72]{2,1,0:T(8,128)(2,1)} %w_value_ref.1) | copy-start | bytes 62212
  37.6 9.5 %copy-start.2 = (bf16[2,72,72]{2,1,0:T(8,128)(2,1)S(1)}, bf16[2,72,72]{2,1,0:T(8,128)(2,1)}, u32[]{:S(2)}) copy-start(bf16[2,72,72]{2,1,0:T(8,128)(2,1)} %w_out_ref.1) | copy-start | bytes 62212
  37.6 9.5 %copy-start.3 = (f32[72,72]{1,0:T(8,128)S(1)}, f32[72,72]{1,0:T(8,128)}, u32[]{:S(2)}) copy-start(f32[72,72]{1,0:T(8,128)} %w_final_ref.1) | copy-start | bytes 62212
  37.6 9.5 %copy-start.4 = (f32[36,72]{1,0:T(8,128)S(1)}, f32[36,72]{1,0:T(8,128)}, u32[]{:S(2)}) copy-start(f32[36,72]{1,0:T(8,128)} %pos_ref.1) | copy-start | bytes 31108
  37.8 9.4 %copy-start.5 = (s32[4,8,16]{2,1,0:T(8,128)S(1)}, s32[4,8,16]{2,1,0:T(8,128)}, u32[]{:S(2)}) copy-start(s32[4,8,16]{2,1,0:T(8,128)} %swap_ref.1) | copy-start | bytes 6148
  38.3 8.9 %copy-start.12 = (bf16[4,64]{1,0:T(4,128)(2,1)S(1)}, bf16[4,64]{1,0:T(4,128)(2,1)}, u32[]{:S(2)}) copy-start(bf16[4,64]{1,0:T(4,128)(2,1)} %constant.27.clone.repeat_ref) | copy-start | bytes 1540
where the time goes:
time: 55.3 us; the launch traced here: 54.9 us
  starting transfers between devices  23.5 us (42%)
  waiting for transfers between devices  17.1 us (31%)
  Pallas kernels  7.68 us (14%)
  local copies, waits for them, and re-layouts  3.59 us (6%)
  other arithmetic  2.18 us (4%)
  between operations  0.88 us (2%)
    all_to_all x1, starting transfers between devices, on_device(): lax.all_to_all(shares, 'grp', 0, 0, tiled=True, axis_index_groups=groups)  13.3 us
    all_to_all x1, waiting for transfers between devices, on_device(): lax.all_to_all(shares, 'grp', 0, 0, tiled=True, axis_index_groups=groups)  8.47 us
    all_to_all x1, waiting for transfers between devices, from_everyone(): lax.all_to_all(jnp.broadcast_to(shard[None], (size, *shard.shape)), axis,...  8.26 us
    all_to_all x1, starting transfers between devices, from_everyone(): lax.all_to_all(jnp.broadcast_to(shard[None], (size, *shard.shape)), axis,...  8.25 us
    pallas_call x1, Pallas kernels, on_device(): prop, spins, amp = replay(*inputs)  7.68 us
    unnamed x43, local copies, waits for them, and re-layouts  2.18 us
    ppermute x1, starting transfers between devices, on_device(): other = lax.ppermute(local_counts, 'grp', [(g, g ^ 1) for g in range(size)])  1.91 us
  transfers between devices with their start and end apart: 3, of which 3 were waited for; matrix products, arithmetic and copies ran while one was open for 3% of the time, Pallas kernels for 0%

commit v1 on v0

--- a/solution.py
+++ b/solution.py
@@ -27,7 +27,7 @@
 ROWS = 96
 SLOT = 8
 HD = HEADS * SLOT
-MSG = SITES + 2 * STEPS
+TAIL = SITES - 128 + 2 * STEPS
 GELU_A = float(np.sqrt(2.0 / np.pi))
 GELU_B = GELU_A * 0.044715
 
@@ -46,23 +46,16 @@
             pick[:, (row * 2 + column) * LANES : (row * 2 + column + 1) * LANES] = (
                 np.arange(SITES)[:, None] == site[None, :]
             ) & used[None, :]
-    pool = (chain[:, None] == np.arange(128)[None, :]) & used[:, None]
     pad = np.zeros((HD, D), np.float32)
     for head in range(HEADS):
         for entry in range(HEAD_DIM):
             pad[head * SLOT + entry, head * HEAD_DIM + entry] = 1.0
-    repeat = np.zeros((4, 64), np.float32)
-    for s in range(4):
-        repeat[s, s * 16 : (s + 1) * 16] = 1.0
     low = jnp.bfloat16
     return (
         jnp.asarray(spread, low),
-        jnp.asarray(spread.T, low),
         jnp.asarray(block, jnp.float32),
         jnp.asarray(pick, low),
-        jnp.asarray(pool, low),
         jnp.asarray(pad, low),
-        jnp.asarray(repeat, low),
     )
 
 
@@ -84,9 +77,34 @@
     return center * lax.rsqrt(spread + 1e-05)
 
 
+def compose(up_hbm, site_hbm, accept_hbm, message_ref, up_ref, site_ref, accept_ref, arrived):
+    f32 = jnp.float32
+    copies = [
+        pltpu.make_async_copy(up_hbm, up_ref, arrived.at[0]),
+        pltpu.make_async_copy(site_hbm, site_ref, arrived.at[1]),
+        pltpu.make_async_copy(accept_hbm, accept_ref, arrived.at[2]),
+    ]
+    for copy in copies:
+        copy.start()
+    for copy in copies:
+        copy.wait()
+    marks = jnp.concatenate([site_ref[...], accept_ref[...]], axis=0).astype(f32).T
+    spins = 2.0 * up_ref[...].astype(f32) - 1.0
+    rest = jnp.concatenate(
+        [spins[:, 128:], marks, jnp.zeros((PLACES, 128 - TAIL), f32)], axis=1
+    )
+    tail = rest[:4]
+    for k in range(1, 4):
+        tail = tail + pltpu.roll(rest[4 * k : 4 * k + 4], 32 * k, 1)
+    for rung in range(RUNGS):
+        for k in range(4):
+            message_ref[rung, :, k * 128 : (k + 1) * 128] = spins[4 * k : 4 * k + 4, :128]
+        message_ref[rung, :, 512:] = tail
+
+
 def kernel(
     bit_hbm,
-    got_ref,
+    sent_ref,
     swap_ref,
     small_ref,
     pos_ref,
@@ -97,12 +115,9 @@
     w_back_ref,
     w_final_ref,
     spread_ref,
-    spread_t_ref,
     block_ref,
     pick_ref,
-    pool_ref,
     pad_ref,
-    repeat_ref,
     prop_ref,
     spins_ref,
     amp_ref,
@@ -122,6 +137,7 @@
     hidden,
     value,
     mixed,
+    got_ref,
     bit_ref,
     arrived,
 ):
@@ -135,7 +151,7 @@
         wv[layer] = mm_t(pad_ref[...], w_value_ref[layer]).astype(low)
         wo[layer] = mm(pad_ref[...], w_out_ref[layer]).T.astype(low)
         wi[layer] = w_in_ref[layer].astype(jnp.float32).T.astype(low)
-        wb[layer] = (0.5 * w_back_ref[layer].astype(jnp.float32)).T.astype(low)
+        wb[layer] = (0.5 * w_back_ref[layer].astype(jnp.float32)).astype(low)
     for layer in range(LAYERS):
         for head in range(HEADS):
             one = mixing_ref[layer, head]
@@ -154,17 +170,24 @@
                 big[layer, head, :, lanes] = jnp.concatenate(tiles, axis=0).astype(low)
 
     copy.wait()
-    embed_x[...] = mm(small_ref[:4].T.astype(low), repeat_ref[...]).astype(low)
+    repeat = lax.broadcasted_iota(jnp.int32, (4, 64), 1) // 16 == lax.broadcasted_iota(jnp.int32, (4, 64), 0)
+    repeat = repeat.astype(jnp.float32).astype(low)
+    embed_x[...] = mm(small_ref[:4].T.astype(low), repeat).astype(low)
 
     column = lax.broadcasted_iota(jnp.int32, (PLACES, SITES), 1).astype(jnp.float32)
     for rung in range(RUNGS):
+        tail = sent_ref[rung, :, 512:]
+        tails = [tail] + [pltpu.roll(tail, 128 - 32 * k, 1) for k in range(1, 4)]
+        heads = [sent_ref[rung, :, k * 128 : (k + 1) * 128] for k in range(4)]
+        got_ref[rung, :, :128] = jnp.concatenate(heads, axis=0)
+        got_ref[rung, :, 128:] = jnp.concatenate(tails, axis=0)
         state[rung] = got_ref[rung, :, :SITES]
     chains[CHAINS:, :] = jnp.zeros((ROWS - CHAINS, SITES), jnp.float32)
     for step in range(STEPS):
         own_site = got_ref[me, :, SITES + step : SITES + step + 1]
         own = state[me]
         chains[step * PLACES : (step + 1) * PLACES, :] = jnp.where(column == own_site, -own, own)
-        bit = bit_ref[step, 0]
+        bit = bit_ref[0, step]
         mask = jnp.left_shift(jnp.int32(1), bit)
         decided = swap_ref[step].T
         for rung in range(RUNGS):
@@ -239,9 +262,12 @@
                 high = x.astype(low)
                 normed[group] = high
                 rests[group] = (x - high.astype(jnp.float32)).astype(low)
+    slots = lax.broadcasted_iota(jnp.int32, (LANES, 128), 1)
+    patch = lax.broadcasted_iota(jnp.int32, (LANES, 128), 0) - PATCHES * slots
+    pool = jnp.where((patch >= 0) & (patch < PATCHES) & (slots < PACK), 1.0, 0.0).astype(low)
     total = jnp.zeros((D, 128), jnp.float32)
     for group in range(GROUPS):
-        part = mm(normed[group], pool_ref[...]) + mm(rests[group], pool_ref[...])
+        part = mm(normed[group], pool) + mm(rests[group], pool)
         total = total + (part if group == 0 else pltpu.roll(part, PACK * group, 1))
 
     eye = lax.broadcasted_iota(jnp.int32, (D, D), 0) == lax.broadcasted_iota(jnp.int32, (D, D), 1)
@@ -253,13 +279,6 @@
     for step in range(STEPS):
         prop_ref[step : step + 1, :] = amps[:, step * PLACES : (step + 1) * PLACES]
     amp_ref[...] = amps[:, STEPS * PLACES : CHAINS]
-
-
-def from_everyone(shard, axis):
-    size = lax.axis_size(axis)
-    return lax.all_to_all(
-        jnp.broadcast_to(shard[None], (size, *shard.shape)), axis, 0, 0, tiled=True
-    )
 
 
 def on_device(
@@ -279,10 +298,21 @@
     b_final,
 ):
     f32, low = jnp.float32, jnp.bfloat16
-    marks = jnp.concatenate([flip_site, accept], axis=0).astype(f32).T
-    message = jnp.concatenate([2.0 * init_up.astype(f32) - 1.0, marks], axis=1)
-    got = from_everyone(message, "ladder")
-    got = got.reshape(RUNGS, PLACES, MSG)
+    vmem = pl.BlockSpec(memory_space=pltpu.VMEM)
+    message = pl.pallas_call(
+        compose,
+        out_shape=jax.ShapeDtypeStruct((RUNGS, 4, 640), f32),
+        in_specs=[pl.BlockSpec(memory_space=pltpu.HBM)] * 3,
+        out_specs=vmem,
+        scratch_shapes=[
+            pltpu.VMEM((PLACES, SITES), jnp.int32),
+            pltpu.VMEM((STEPS, PLACES), jnp.int32),
+            pltpu.VMEM((STEPS, PLACES), jnp.int32),
+            pltpu.SemaphoreType.DMA((3,)),
+        ],
+        compiler_params=pltpu.CompilerParams(vmem_limit_bytes=67000000),
+    )(init_up, flip_site, accept)
+    got = lax.all_to_all(message, "ladder", 0, 0, tiled=True)
     local_counts = jnp.sum(accept.astype(f32), axis=1)
     vmem = pl.BlockSpec(memory_space=pltpu.VMEM)
     hbm = pl.BlockSpec(memory_space=pltpu.HBM)
@@ -293,7 +323,7 @@
             jax.ShapeDtypeStruct((PLACES, SITES), f32),
             jax.ShapeDtypeStruct((1, PLACES), f32),
         ),
-        in_specs=[hbm] + [vmem] * 17,
+        in_specs=[hbm] + [vmem] * 14,
         out_specs=(vmem, vmem, vmem),
         scratch_shapes=[
             pltpu.VMEM((RUNGS, PLACES, SITES), f32),
@@ -312,7 +342,8 @@
             pltpu.VMEM((GROUPS, HID, LANES), low),
             pltpu.VMEM((HEADS, ROWS, LANES), low),
             pltpu.VMEM((GROUPS, HD, LANES), low),
-            pltpu.SMEM((STEPS, 1), jnp.int32),
+            pltpu.VMEM((RUNGS, PLACES, 256), f32),
+            pltpu.SMEM((1, STEPS), jnp.int32),
             pltpu.SemaphoreType.DMA,
         ],
         compiler_params=pltpu.CompilerParams(vmem_limit_bytes=40 * 1024 * 1024),
@@ -320,7 +351,7 @@
     )
     small = jnp.concatenate([w_embed.astype(f32), b_final[None]], axis=0)
     inputs = (
-        ladder_bit,
+        ladder_bit.T,
         got,
         swap_ok,
         small,
@@ -329,7 +360,7 @@
         mixing,
         w_out,
         w_in,
-        w_back,
+        jnp.swapaxes(w_back, 1, 2),
         w_final,
         *constants(),
     )

time: 55.3 us -> 53.7 us (0.971)
  Pallas kernels: 7.68 us -> 9.04 us
  local copies, waits for them, and re-layouts: 3.59 us -> 2.43 us
  waiting for transfers between devices: 17.1 us -> 16.1 us
  other arithmetic: 2.18 us -> 1.36 us
    pallas_call x0 -> x1, Pallas kernels: none -> 1.63 us  [on_device(): pl.pallas_call(compose, out_shape=jax.ShapeDtypeStruct((RUNGS, 4, 640), f...]
    all_to_all x1, waiting for transfers between devices: 8.47 us -> 6.9 us  [on_device(): lax.all_to_all(shares, 'grp', 0, 0, tiled=True, axis_index_groups=groups)]
    ppermute x1, waiting for transfers between devices: 0.33 us -> 1.13 us  [on_device(): other = lax.ppermute(local_counts, 'grp', [(g, g ^ 1) for g in range(size)])]
    broadcast_in_dim x1 -> x0, local copies, waits for them, and re-layouts: 0.73 us -> none  [from_everyone(): jnp.broadcast_to(shard[None], (size, *shard.shape))]
    transpose x1 -> x0, other arithmetic: 0.69 us -> none  [on_device(): marks = jnp.concatenate([flip_site, accept], axis=0).astype(f32).T]
    unnamed x43 -> x29, local copies, waits for them, and re-layouts: 2.18 us -> 1.82 us
  transfers between devices with their start and end apart: 3 -> 3, of which waited for: 3 -> 3; matrix products, arithmetic and copies ran while one was open for 3% -> 3% of each run, Pallas kernels for 0% -> 3%
where the time goes in v1:
time: 53.7 us; the launch traced here: 53.3 us
  starting transfers between devices  23.5 us (44%)
  waiting for transfers between devices  16.1 us (30%)
  Pallas kernels  9.04 us (17%)
  local copies, waits for them, and re-layouts  2.43 us (5%)
  other arithmetic  1.36 us (3%)
  between operations  0.85 us (2%)
    all_to_all x1, starting transfers between devices, on_device(): lax.all_to_all(shares, 'grp', 0, 0, tiled=True, axis_index_groups=groups)  13.3 us
    all_to_all x1, starting transfers between devices, on_device(): got = lax.all_to_all(message, 'ladder', 0, 0, tiled=True)  8.25 us
    all_to_all x1, waiting for transfers between devices, on_device(): got = lax.all_to_all(message, 'ladder', 0, 0, tiled=True)  8.1 us
    pallas_call x1, Pallas kernels, on_device(): prop, spins, amp = replay(*inputs)  7.41 us
    all_to_all x1, waiting for transfers between devices, on_device(): lax.all_to_all(shares, 'grp', 0, 0, tiled=True, axis_index_groups=groups)  6.9 us
    ppermute x1, starting transfers between devices, on_device(): other = lax.ppermute(local_counts, 'grp', [(g, g ^ 1) for g in range(size)])  1.91 us
    unnamed x29, local copies, waits for them, and re-layouts  1.82 us
    pallas_call x1, Pallas kernels, on_device(): pl.pallas_call(compose, out_shape=jax.ShapeDtypeStruct((RUNGS, 4, 640), f...  1.63 us
  transfers between devices with their start and end apart: 3, of which 3 were waited for; matrix products, arithmetic and copies ran while one was open for 3% of the time, Pallas kernels for 3%

profile of v1, /device:TPU:2, one launch (start us, length us, event | category | flops | bytes accessed | tf_op | source)
XLA Modules:
  0.0 53.3 jit_solution(2800338389498055877)
XLA Ops:
  0.6 0.8 %convert_reduce_fusion = f32[4]{0:T(128)S(1)} fusion(s32[4,16]{1,0:T(4,128)} %accept_hbm.1), kind=kLoop, calls=%fused_computation.1 | loop fusion | flops 124 | bytes 272 | tf_op jit(solution)/shard_map/reduce_sum | solution.py:316
  1.4 1.9 %collective-permute-start = (f32[4]{0:T(128)S(1)}, f32[4]{0:T(128)S(1)}, u32[]{:S(2)}, u32[]{:S(2)}) collective-permute-start(f32[4]{0:T(128)S(1)} %convert_reduce_fusion), channel_id=1, source_target_pairs={{0,1},{1,0},{2,3},{3,2},{4,5},{5,4},{6,7},{7,6},{8,9},{9,8},{10,11... | collective-permute-start | bytes 56 | tf_op jit(solution)/shard_map/ppermute | solution.py:369
  3.3 1.1 %collective-permute-done = f32[4]{0:T(128)S(1)} collective-permute-done((f32[4]{0:T(128)S(1)}, f32[4]{0:T(128)S(1)}, u32[]{:S(2)}, u32[]{:S(2)}) %collective-permute-start) | collective-permute-done | bytes 48 | tf_op jit(solution)/shard_map/ppermute | solution.py:369
  4.5 0.6 %broadcast_in_dim.10 = f32[16,1,4]{2,1,0:T(1,128)} broadcast(f32[4]{0:T(128)S(1)} %add.3), dimensions={2} | broadcast | bytes 272 | tf_op jit(solution)/shard_map/broadcast_in_dim | solution.py:371
  5.1 13.3 %all-to-all-start.1 = ((f32[16,1,4]{2,1,0:T(1,128)}), f32[16,1,4]{2,1,0:T(1,128)S(1)}, u32[]{:S(2)}, u32[]{:S(2)}) async-start(f32[16,1,4]{2,1,0:T(1,128)} %broadcast_in_dim.10), calls=%async_computation.1 | async-start | bytes 16384 | tf_op jit(solution)/shard_map/all_to_all | solution.py:373
  18.4 1.6 %shard_map.201 = f32[16,4,640]{2,1,0:T(4,128)} custom-call(s32[16,144]{1,0:T(8,128)} %up_hbm.1, s32[4,16]{1,0:T(4,128)} %site_hbm.1, s32[4,16]{1,0:T(4,128)} %accept_hbm.1), custom_call_target="tpu_custom_call" | custom-call | tf_op jit(solution)/shard_map/pallas_call | solution.py:302
  20.0 0.0 copy-start.12
  20.0 6.9 %all-to-all-done.1 = f32[16,1,4]{2,1,0:T(1,128)S(1)} async-done(((f32[16,1,4]{2,1,0:T(1,128)}), f32[16,1,4]{2,1,0:T(1,128)S(1)}, u32[]{:S(2)}, u32[]{:S(2)}) %all-to-all-start.1) | async-done | bytes 288 | tf_op jit(solution)/shard_map/all_to_all | solution.py:373
  26.9 0.0 copy-start.11
  27.0 8.2 %all-to-all-start = ((f32[16,4,640]{2,1,0:T(4,128)}), f32[16,4,640]{2,1,0:T(4,128)S(1)}, u32[]{:S(2)}, u32[]{:S(2)}) async-start(f32[16,4,640]{2,1,0:T(4,128)} %shard_map.201), calls=%async_computation | async-start | bytes 327680 | tf_op jit(solution)/shard_map/all_to_all | solution.py:315
  35.2 0.0 copy-done.12
  35.2 0.0 copy-start.13
  35.2 0.0 copy-start
  35.3 0.0 copy-start.1
  35.3 0.0 copy-start.2
  35.3 0.0 copy-start.3
  35.3 0.0 copy-start.4
  35.3 0.0 copy-start.6
  35.3 0.0 copy-start.8
  35.3 0.0 copy-start.9
  35.3 0.0 copy-start.10
  35.4 1.2 %copy.24.mixing_ref = f32[2,12,36,36]{3,2,1,0:T(8,128)S(1)} copy(f32[2,12,36,36]{3,0,2,1:T(2,128)} %param.26) | data formatting | bytes 248832 | tf_op args[8]
  36.5 0.0 copy-start.5
  36.5 0.0 copy-done.13
  36.6 0.5 %reduce_sum.19 = f32[4]{0:T(128)} reduce(f32[16,1,4]{2,1,0:T(1,128)S(1)} %all-to-all-done.1, f32[]{:T(128)} %constant.4.clone.1), dimensions={0,1}, to_apply=%region_1.0 | reduce | flops 60 | bytes 276 | tf_op jit(solution)/shard_map/reduce_sum | solution.py:374
  37.1 8.1 %all-to-all-done.sent_ref = f32[16,4,640]{2,1,0:T(4,128)S(1)} async-done(((f32[16,4,640]{2,1,0:T(4,128)}), f32[16,4,640]{2,1,0:T(4,128)S(1)}, u32[]{:S(2)}, u32[]{:S(2)}) %all-to-all-start) | async-done | bytes 163872 | tf_op jit(solution)/shard_map/all_to_all | solution.py:315
  45.2 0.0 copy-start.7
  45.2 0.0 copy-done.11
  45.2 0.0 copy-done
  45.2 0.0 copy-done.1
  45.2 0.0 copy-done.2
  45.2 0.0 copy-done.3
  45.3 0.0 copy-done.4
  45.3 0.0 copy-done.6
  45.3 0.0 copy-done.8
  45.3 0.0 copy-done.9
  45.3 0.0 copy-done.10
  45.3 0.0 copy-done.5
  45.3 0.6 %copy-done.7 = s32[4,1]{0,1:T(1,128)S(1)} copy-done((s32[4,1]{0,1:T(1,128)S(1)}, s32[4,1]{0,1:T(1,128)}, u32[]{:S(2)}) %copy-start.7) | copy-done | bytes 40
  45.9 7.4 %shard_map.202 = (f32[4,16]{1,0:T(4,128)}, f32[16,144]{1,0:T(8,128)}, f32[1,16]{1,0:T(1,128)}) custom-call(s32[1,4]{1,0:T(1,128)S(1)} %bitcast.6, f32[16,4,640]{2,1,0:T(4,128)S(1)} %all-to-all-done.sent_ref, s32[4,8,16]{2,1,0:T(8,128)S(1)} %copy-done.6, f32[5,72]{1,0:T(8,128)S(1)} %pad_maximum_fusion.small_ref, f32[36,72]{1,0:T(8,128)S(1)} %copy-done.5, ...), custom_call_target="tpu_custom_call" | custom-call | flops 2000000000 | bytes 1000000 | tf_op jit(solution)/shard_map/pallas_call | solution.py:367
  (3 shorter events, 0.0 us)
Async XLA Ops:
  1.4 3.0 %collective-permute-start = (f32[4]{0:T(128)S(1)}, f32[4]{0:T(128)S(1)}, u32[]{:S(2)}, u32[]{:S(2)}) collective-permute-start(f32[4]{0:T(128)S(1)} %convert_reduce_fusion), channel_id=1, source_target_pairs={{0,1},{1,0},{2,3},{3,2},{4,5},{5,4},{6,7},{7,6},{8,9},{9,8},{10,11... | collective-permute-start | bytes 56 | tf_op jit(solution)/shard_map/ppermute | solution.py:369
  5.1 21.9 %all-to-all-start.1 = ((f32[16,1,4]{2,1,0:T(1,128)}), f32[16,1,4]{2,1,0:T(1,128)S(1)}, u32[]{:S(2)}, u32[]{:S(2)}) async-start(f32[16,1,4]{2,1,0:T(1,128)} %broadcast_in_dim.10), calls=%async_computation.1 | async-start | bytes 16384 | tf_op jit(solution)/shard_map/all_to_all | solution.py:373
  20.0 15.2 %copy-start.12 = (bf16[4,72]{1,0:T(4,128)(2,1)S(1)}, bf16[4,72]{1,0:T(4,128)(2,1)}, u32[]{:S(2)}) copy-start(bf16[4,72]{1,0:T(4,128)(2,1)} %param.23) | copy-start | bytes 1732
  26.9 18.3 %copy-start.11 = (bf16[36,256]{1,0:T(8,128)(2,1)S(1)}, bf16[36,256]{1,0:T(8,128)(2,1)}, u32[]{:S(2)}) copy-start(bf16[36,256]{1,0:T(8,128)(2,1)} %constant.10.clone.spread_ref) | copy-start | bytes 55300
  27.0 18.3 %all-to-all-start = ((f32[16,4,640]{2,1,0:T(4,128)}), f32[16,4,640]{2,1,0:T(4,128)S(1)}, u32[]{:S(2)}, u32[]{:S(2)}) async-start(f32[16,4,640]{2,1,0:T(4,128)} %shard_map.201), calls=%async_computation | async-start | bytes 327680 | tf_op jit(solution)/shard_map/all_to_all | solution.py:315
  35.2 1.3 %copy-start.13 = (f32[72]{0:T(128)S(1)}, f32[72]{0:T(128)}, u32[]{:S(2)}) copy-start(f32[72]{0:T(128)} %param.31) | copy-start | bytes 868
  35.2 10.0 %copy-start = (bf16[2,72,288]{2,1,0:T(8,128)(2,1)S(1)}, bf16[2,72,288]{2,1,0:T(8,128)(2,1)}, u32[]{:S(2)}) copy-start(bf16[2,72,288]{2,1,0:T(8,128)(2,1)} %w_in_ref.1) | copy-start | bytes 248836
  35.3 10.0 %copy-start.1 = (bf16[2,288,72]{1,2,0:T(8,128)(2,1)S(1)}, bf16[2,288,72]{1,2,0:T(8,128)(2,1)}, u32[]{:S(2)}) copy-start(bf16[2,288,72]{1,2,0:T(8,128)(2,1)} %param.29) | copy-start | bytes 248836
  35.3 10.0 %copy-start.2 = (bf16[2,72,72]{2,1,0:T(8,128)(2,1)S(1)}, bf16[2,72,72]{2,1,0:T(8,128)(2,1)}, u32[]{:S(2)}) copy-start(bf16[2,72,72]{2,1,0:T(8,128)(2,1)} %w_value_ref.1) | copy-start | bytes 62212
  35.3 10.0 %copy-start.3 = (bf16[2,72,72]{2,1,0:T(8,128)(2,1)S(1)}, bf16[2,72,72]{2,1,0:T(8,128)(2,1)}, u32[]{:S(2)}) copy-start(bf16[2,72,72]{2,1,0:T(8,128)(2,1)} %w_out_ref.1) | copy-start | bytes 62212
  35.3 10.0 %copy-start.4 = (f32[72,72]{1,0:T(8,128)S(1)}, f32[72,72]{1,0:T(8,128)}, u32[]{:S(2)}) copy-start(f32[72,72]{1,0:T(8,128)} %w_final_ref.1) | copy-start | bytes 62212
  35.3 10.0 %copy-start.6 = (s32[4,8,16]{2,1,0:T(8,128)S(1)}, s32[4,8,16]{2,1,0:T(8,128)}, u32[]{:S(2)}) copy-start(s32[4,8,16]{2,1,0:T(8,128)} %swap_ref.1) | copy-start | bytes 6148
  35.3 10.0 %copy-start.8 = (bf16[144,1024]{1,0:T(8,128)(2,1)S(1)}, bf16[144,1024]{1,0:T(8,128)(2,1)}, u32[]{:S(2)}) copy-start(bf16[144,1024]{1,0:T(8,128)(2,1)} %constant.12.clone.pick_ref) | copy-start | bytes 884740
  35.3 10.0 %copy-start.9 = (f32[256,256]{1,0:T(8,128)S(1)}, f32[256,256]{1,0:T(8,128)}, u32[]{:S(2)}) copy-start(f32[256,256]{1,0:T(8,128)} %constant.11.clone.block_ref) | copy-start | bytes 786436
  35.3 10.0 %copy-start.10 = (bf16[96,72]{1,0:T(8,128)(2,1)S(1)}, bf16[96,72]{1,0:T(8,128)(2,1)}, u32[]{:S(2)}) copy-start(bf16[96,72]{1,0:T(8,128)(2,1)} %constant.13.clone.pad_ref) | copy-start | bytes 41476
  36.5 8.8 %copy-start.5 = (f32[36,72]{1,0:T(8,128)S(1)}, f32[36,72]{1,0:T(8,128)}, u32[]{:S(2)}) copy-start(f32[36,72]{1,0:T(8,128)} %pos_ref.1) | copy-start | bytes 31108
  45.2 0.7 %copy-start.7 = (s32[4,1]{0,1:T(1,128)S(1)}, s32[4,1]{0,1:T(1,128)}, u32[]{:S(2)}) copy-start(s32[4,1]{0,1:T(1,128)} %param.22) | copy-start | bytes 52
